TPU v7x, 32 devices: a whole 2x2x4 slice. The times are simulated.
32 devices in a mesh: epoch: 8 (over z, y), blend: 4 (over x, core).
Axes of the slice: x: 2, y: 2, z: 4, core: 2. Of those that a mesh axis runs over, the one named last changes fastest.
Arguments:
- models: float32 [4, 16, 6, 4096], P('blend', 'epoch'), may hold values from -6 to 6
- observed: bfloat16 [8, 64, 4096], P('epoch', 'blend'), may hold values from -6 to 6
- weights: float32 [8, 64], P('epoch', 'blend'), may hold values from 0.5 to 2
- coverage: int32 [8, 64], P('epoch', 'blend'), may hold values from 0 to 1, as said below
- offsets: int32 [8, 64, 2], P('epoch', 'blend'), may hold values from 0 to 63
- counts: int32 [4, 16], P('blend', 'epoch'), may hold values from 1 to 8, as said below
- psf_y: bfloat16 [8, 4096], P('epoch'), may hold values from -0.75 to 0.75
- resample_y: bfloat16 [8, 4096], P('epoch'), may hold values from -0.75 to 0.75
- psf_x: bfloat16 [8, 4096], P('epoch'), may hold values from -0.75 to 0.75
- resample_x: bfloat16 [8, 4096], P('epoch'), may hold values from -0.75 to 0.75
Outputs:
- updated: float32 [4, 16, 6, 4096], P('blend', 'epoch')
Inputs may be any that keep to these rules, and one draw needn't show every extreme that they name: `coverage`: every blend is seen by one epoch or more. counts of blend b is the sum of coverage over all epochs for b.
All inputs are finite; a program needn't handle non-finite values.
Results may differ from a plain program's by a relative error of at most 0.0017.
Values may be sent and summed in bfloat16 or wider, within the bound.
A program may use at most 128 MiB of HBM per device.

v0:
```python
import jax
import jax.numpy as jnp
from jax import lax
from jax.sharding import PartitionSpec as P

CUT = 64
BANDS = 6
PIX2 = 4096
step_size = 0.5


def roll_forward(image, down, across):
    side = image.shape[0]
    doubled = jnp.concatenate([image, image], axis=0)
    rows = lax.dynamic_slice_in_dim(doubled, down, side, 0)
    doubled = jnp.concatenate([rows, rows], axis=1)
    return lax.dynamic_slice_in_dim(doubled, across, side, 1)


def one_epoch(model_low, observed, scale, offsets, left, right, band):
    side = left.shape[0]
    count = observed.shape[0]
    chosen = lax.dynamic_index_in_dim(model_low, band, 1, keepdims=False)
    shifted = jax.vmap(roll_forward)(chosen, offsets[:, 0], offsets[:, 1])
    blurred = jnp.einsum("ij,bjk->bik", left, shifted, preferred_element_type=jnp.float32).astype(
        jnp.bfloat16
    )
    predicted = jnp.einsum("bik,lk->bil", blurred, right, preferred_element_type=jnp.float32)
    target = observed.reshape(count, side, side).astype(jnp.float32)
    misfit = (scale[:, None, None] * (predicted - target)).astype(jnp.bfloat16)
    back = jnp.einsum("ji,bjk->bik", left, misfit, preferred_element_type=jnp.float32).astype(
        jnp.bfloat16
    )
    term = jnp.einsum("bik,kl->bil", back, right, preferred_element_type=jnp.float32)
    return jax.vmap(roll_forward)(term, side - offsets[:, 0], side - offsets[:, 1])


def on_device(
    models, observed, weights, coverage, offsets, counts, psf_y, resample_y, psf_x, resample_x
):
    ep_dev = observed.shape[0]
    group_size = lax.axis_size("epoch")
    all_epochs = ep_dev * group_size
    anchor = lax.axis_index("epoch") * ep_dev
    lefts = jnp.einsum(
        "eij,ejk->eik",
        psf_y.reshape(ep_dev, CUT, CUT),
        resample_y.reshape(ep_dev, CUT, CUT),
        preferred_element_type=jnp.float32,
    ).astype(jnp.bfloat16)
    rights = jnp.einsum(
        "eij,ejk->eik",
        psf_x.reshape(ep_dev, CUT, CUT),
        resample_x.reshape(ep_dev, CUT, CUT),
        preferred_element_type=jnp.float32,
    ).astype(jnp.bfloat16)
    scale = weights * coverage.astype(jnp.float32)
    epoch_bands = (anchor + 0) * BANDS // all_epochs
    first_band = anchor * BANDS // all_epochs
    model_low = models.astype(jnp.bfloat16)
    piece = lax.all_gather(model_low, "epoch", axis=1, tiled=True)
    count = piece.shape[1]
    blocks = piece[0].reshape(count, BANDS, CUT, CUT)
    terms = one_epoch(
        blocks, observed[0], scale[0], offsets[0], lefts[0], rights[0], epoch_bands
    ).reshape(count, PIX2)
    total = jnp.zeros((count, 2, PIX2), jnp.float32)
    slot = epoch_bands - first_band
    current = lax.dynamic_index_in_dim(total, slot, 1, keepdims=False)
    total = lax.dynamic_update_index_in_dim(total, current + terms, slot, 1)
    received = lax.all_to_all(total, "epoch", split_axis=0, concat_axis=1, tiled=True)
    slot_count = received.shape[1]
    position = jnp.arange(slot_count, dtype=jnp.int32)
    source = position // 2
    band_of = source * ep_dev * BANDS // all_epochs + position % 2
    selector = (band_of[:, None] == jnp.arange(BANDS, dtype=jnp.int32)[None, :]).astype(jnp.float32)
    gradient = jnp.einsum("bkp,kc->bcp", received, selector, precision=lax.Precision.HIGHEST)
    divisor = counts[0].astype(jnp.float32)[:, None, None]
    updated = models[0] - step_size * gradient / divisor
    return updated[None]


def solution(mesh):
    return jax.shard_map(
        on_device,
        mesh=mesh,
        in_specs=(
            P("blend", "epoch", None, None),
            P("epoch", "blend", None),
            P("epoch", "blend"),
            P("epoch", "blend"),
            P("epoch", "blend", None),
            P("blend", "epoch"),
            P("epoch", None),
            P("epoch", None),
            P("epoch", None),
            P("epoch", None),
        ),
        out_specs=P("blend", "epoch", None, None),
        check_vma=False,
    )
```

profile of v0, /device:TPU:0, one launch (start us, length us, event | category | flops | bytes accessed | tf_op | source)
XLA Modules:
  0.0 66.9 jit_solution(17146201242047359278)
XLA Ops:
  0.0 1.0 %convert_element_type.47 = bf16[1,2,6,4096]{3,1,2,0:T(2,128)(2,1)S(1)} convert(f32[1,2,6,4096]{3,1,2,0:T(2,128)} %param.10) | non-fusion elementwise | flops 49152 | bytes 294912 | tf_op jit(solution)/shard_map/convert_element_type | solution.py:60
  1.0 0.1 copy.60
  1.1 34.6 %all_gather.3 = bf16[1,16,6,4096]{3,2,0,1:T(8,128)(2,1)S(1)} all-gather(bf16[1,2,6,4096]{3,2,0,1:T(8,128)(2,1)S(1)} %copy.60), channel_id=1, replica_groups=mesh['epoch'=8,'blend'=4] {'epoch'}, dimensions={1}, use_global_device_ids=true | all-gather | bytes 884736 | tf_op jit(solution)/shard_map/all_gather | solution.py:61
  35.7 0.4 copy.61
  36.1 0.0 copy-start.6
  36.1 1.7 %reshape_squeeze.4 = bf16[16,6,64,64]{3,2,0,1:T(8,128)(2,1)S(1)} reshape(bf16[1,16,6,4096]{3,1,2,0:T(8,128)(2,1)S(1)} %copy.61) | data formatting | bytes 1572864 | tf_op jit(solution)/shard_map/reshape;squeeze | solution.py:63
  37.9 0.2 copy.86
  38.1 0.1 pad_maximum_fusion
  38.2 0.0 copy-done.6
  38.2 0.0 copy-start.2
  38.2 0.0 copy-start.3
  38.2 0.0 copy-start.4
  38.2 0.0 copy-start.5
  38.3 0.0 copy-start.1
  38.3 1.4 %gather_fusion = bf16[16,64,64]{2,0,1:T(8,128)(2,1)S(1)} fusion(bf16[16,128,64]{2,0,1:T(8,128)(2,1)S(1)} %pad_maximum_fusion, s32[16]{0:T(128)S(1)} %get-tuple-element.6), kind=kCustom, calls=%fused_computation | custom fusion | bytes 262336 | tf_op jit(solution)/shard_map/vmap()/gather | solution.py:15
  39.6 0.1 pad_maximum_fusion.3
  39.8 0.5 copy.63
  40.4 0.1 reduce.2
  40.4 0.1 reshape.76
  40.5 0.1 reduce.3
  40.5 0.1 reshape.77
  40.6 0.1 reduce
  40.7 0.1 reshape.74
  40.8 0.1 reduce.1
  40.8 0.0 copy-start.7
  40.8 0.0 copy-start.8
  40.9 0.1 reshape.75
  40.9 0.2 reshape.78
  41.2 1.4 %gather_fusion.1 = bf16[16,64,64]{1,0,2:T(8,128)(2,1)S(1)} fusion(bf16[16,64,128]{1,0,2:T(8,128)(2,1)S(1)} %copy.63, s32[16]{0:T(128)S(1)} %get-tuple-element.7), kind=kCustom, calls=%fused_computation.1 | custom fusion | bytes 262336 | tf_op jit(solution)/shard_map/vmap()/gather | solution.py:17
  42.5 0.1 fusion.10
  42.7 0.1 fusion.9
  42.8 0.4 fusion.5
  43.3 0.4 fusion.8
  43.7 0.2 pad_maximum_fusion.1
  43.9 0.5 copy.69
  44.4 1.3 %gather_fusion.2 = f32[16,64,64]{2,0,1:T(8,128)S(1)} fusion(f32[16,128,64]{2,0,1:T(8,128)S(1)} %copy.69, s32[16]{0:T(128)S(1)} %get-tuple-element.8), kind=kCustom, calls=%fused_computation.2 | custom fusion | bytes 524480 | tf_op jit(solution)/shard_map/vmap()/gather | solution.py:15
  45.8 0.2 pad_maximum_fusion.2
  46.0 0.6 copy.70
  46.6 1.3 %gather_fusion.3 = f32[16,64,64]{1,0,2:T(8,128)S(1)} fusion(f32[16,64,128]{1,0,2:T(8,128)S(1)} %copy.70, s32[16]{0:T(128)S(1)} %get-tuple-element.5), kind=kCustom, calls=%fused_computation.3 | custom fusion | bytes 524480 | tf_op jit(solution)/shard_map/vmap()/gather | solution.py:17
  47.9 0.3 copy.71
  48.2 0.0 copy-start.9
  48.2 0.3 broadcast_in_dim.8
  48.5 1.0 %dynamic_update_slice.4.clone = f32[16,2,4096]{2,1,0:T(2,128)} pad(f32[16,1,4096]{2,1,0:T(1,128)S(1)} %broadcast_in_dim.8, f32[]{:T(128)} %constant.85.clone.1), padding=0_0x0_1x0_0 | pad | bytes 786436 | tf_op jit(solution)/shard_map/jit(dynamic_update_index_in_dim)/dynamic_update_slice | solution.py:70
  49.5 5.5 %all-to-all-start = ((f32[16,2,4096]{2,1,0:T(2,128)}), f32[16,2,4096]{2,1,0:T(2,128)S(1)}, u32[]{:S(2)}, u32[]{:S(2)}) async-start(f32[16,2,4096]{2,1,0:T(2,128)} %dynamic_update_slice.4.clone), calls=%async_computation | async-start | bytes 1048576 | tf_op jit(solution)/shard_map/all_to_all | solution.py:71
  55.0 10.3 %all-to-all-done = f32[16,2,4096]{2,1,0:T(2,128)S(1)} async-done(((f32[16,2,4096]{2,1,0:T(2,128)}), f32[16,2,4096]{2,1,0:T(2,128)S(1)}, u32[]{:S(2)}, u32[]{:S(2)}) %all-to-all-start) | async-done | bytes 524320 | tf_op jit(solution)/shard_map/all_to_all | solution.py:71
  65.3 0.4 all_to_all.16
  65.7 0.4 fusion.3
  66.1 0.8 %copy.74 = f32[1,2,6,4096]{3,1,2,0:T(2,128)} copy(f32[1,2,6,4096]{3,2,1,0:T(8,128)S(1)} %fusion.3) | data formatting | bytes 393216 | tf_op jit(solution)/shard_map/broadcast_in_dim | solution.py:80
  (16 shorter events, 0.1 us)
Async XLA Ops:
  36.1 2.1 %copy-start.6 = (s32[1,16,2]{1,2,0:T(2,128)S(1)}, s32[1,16,2]{1,2,0:T(2,128)}, u32[]{:S(2)}) copy-start(s32[1,16,2]{1,2,0:T(2,128)} %param.14) | copy-start | bytes 388
  38.2 2.1 %copy-start.2 = (bf16[1,4096]{1,0:T(2,128)(2,1)S(1)}, bf16[1,4096]{1,0:T(2,128)(2,1)}, u32[]{:S(2)}) copy-start(bf16[1,4096]{1,0:T(2,128)(2,1)} %param.18) | copy-start | bytes 24580
  38.2 2.3 %copy-start.3 = (bf16[1,4096]{1,0:T(2,128)(2,1)S(1)}, bf16[1,4096]{1,0:T(2,128)(2,1)}, u32[]{:S(2)}) copy-start(bf16[1,4096]{1,0:T(2,128)(2,1)} %param.19) | copy-start | bytes 24580
  38.2 2.4 %copy-start.4 = (bf16[1,4096]{1,0:T(2,128)(2,1)S(1)}, bf16[1,4096]{1,0:T(2,128)(2,1)}, u32[]{:S(2)}) copy-start(bf16[1,4096]{1,0:T(2,128)(2,1)} %param.16) | copy-start | bytes 24580
  38.2 2.5 %copy-start.5 = (bf16[1,4096]{1,0:T(2,128)(2,1)S(1)}, bf16[1,4096]{1,0:T(2,128)(2,1)}, u32[]{:S(2)}) copy-start(bf16[1,4096]{1,0:T(2,128)(2,1)} %param.17) | copy-start | bytes 24580
  38.3 2.7 %copy-start.1 = (bf16[1,16,4096]{2,1,0:T(8,128)(2,1)S(1)}, bf16[1,16,4096]{2,1,0:T(8,128)(2,1)}, u32[]{:S(2)}) copy-start(bf16[1,16,4096]{2,1,0:T(8,128)(2,1)} %param.11) | copy-start | bytes 393220
  40.8 2.0 %copy-start.7 = (f32[1,16]{1,0:T(1,128)S(1)}, f32[1,16]{1,0:T(1,128)}, u32[]{:S(2)}) copy-start(f32[1,16]{1,0:T(1,128)} %param.12) | copy-start | bytes 196
  40.8 1.9 %copy-start.8 = (s32[1,16]{1,0:T(1,128)S(1)}, s32[1,16]{1,0:T(1,128)}, u32[]{:S(2)}) copy-start(s32[1,16]{1,0:T(1,128)} %param.13) | copy-start | bytes 196
  48.2 6.9 %copy-start.9 = (s32[1,2]{1,0:T(1,128)S(1)}, s32[1,2]{1,0:T(1,128)}, u32[]{:S(2)}) copy-start(s32[1,2]{1,0:T(1,128)} %param.15) | copy-start | bytes 28
  49.5 16.2 %copy-start = (f32[1,2,6,4096]{3,1,2,0:T(2,128)S(1)}, f32[1,2,6,4096]{3,1,2,0:T(2,128)}, u32[]{:S(2)}) copy-start(f32[1,2,6,4096]{3,1,2,0:T(2,128)} %param.10) | copy-start | bytes 589828
  49.5 15.8 %all-to-all-start = ((f32[16,2,4096]{2,1,0:T(2,128)}), f32[16,2,4096]{2,1,0:T(2,128)S(1)}, u32[]{:S(2)}, u32[]{:S(2)}) async-start(f32[16,2,4096]{2,1,0:T(2,128)} %dynamic_update_slice.4.clone), calls=%async_computation | async-start | bytes 1048576 | tf_op jit(solution)/shard_map/all_to_all | solution.py:71
where the time goes:
time: 67.1 us; the launch traced here: 66.9 us
  blocking collectives  34.6 us (52%)
  local copies, waits for them, and re-layouts  12.8 us (19%)
  waiting for transfers between devices  10.3 us (15%)
  starting transfers between devices  5.52 us (8%)
  other arithmetic  1.9 us (3%)
  matrix products  1.48 us (2%)
    all_gather x1, blocking collectives, on_device(): piece = lax.all_gather(model_low, 'epoch', axis=1, tiled=True)  34.6 us
    all_to_all x1, waiting for transfers between devices, on_device(): lax.all_to_all(total, 'epoch', split_axis=0, concat_axis=1, tiled=True)  10.3 us
    all_to_all x1, starting transfers between devices, on_device(): lax.all_to_all(total, 'epoch', split_axis=0, concat_axis=1, tiled=True)  5.52 us
    gather x3, local copies, waits for them, and re-layouts, roll_forward(): return lax.dynamic_slice_in_dim(doubled, across, side, 1)  2.97 us
    gather x2, local copies, waits for them, and re-layouts, roll_forward(): rows = lax.dynamic_slice_in_dim(doubled, down, side, 0)  2.71 us
    another operation x1, local copies, waits for them, and re-layouts, on_device(): blocks = piece[0].reshape(count, BANDS, CUT, CUT)  1.72 us
  transfers between devices with their start and end apart: 1, of which 1 were waited for; matrix products, arithmetic and copies ran while one was open for 0% of the time, Pallas kernels for 0%

commit v1 on v0

--- a/solution.py
+++ b/solution.py
@@ -68,7 +68,8 @@
     slot = epoch_bands - first_band
     current = lax.dynamic_index_in_dim(total, slot, 1, keepdims=False)
     total = lax.dynamic_update_index_in_dim(total, current + terms, slot, 1)
-    received = lax.all_to_all(total, "epoch", split_axis=0, concat_axis=1, tiled=True)
+    heard = jnp.stack(jnp.split(total, lax.axis_size("epoch"), axis=0))
+    received = jnp.concatenate(lax.all_to_all(heard, "epoch", 0, 0), axis=1)
     slot_count = received.shape[1]
     position = jnp.arange(slot_count, dtype=jnp.int32)
     source = position // 2

time: 67.1 us -> 70.9 us (1.057)
  local copies, waits for them, and re-layouts: 12.8 us -> 16.4 us
    unnamed x20 -> x27, local copies, waits for them, and re-layouts: 0.06 us -> 4.53 us
    dynamic_update_slice x1 -> x0, local copies, waits for them, and re-layouts: 0.99 us -> none  [on_device(): total = lax.dynamic_update_index_in_dim(total, current + terms, slot, 1)]
where the time goes in v1:
time: 70.9 us; the launch traced here: 70.6 us
  blocking collectives  34.6 us (49%)
  local copies, waits for them, and re-layouts  16.4 us (23%)
  waiting for transfers between devices  10.3 us (15%)
  starting transfers between devices  5.39 us (8%)
  other arithmetic  1.9 us (3%)
  matrix products  1.78 us (3%)
    all_gather x1, blocking collectives, on_device(): piece = lax.all_gather(model_low, 'epoch', axis=1, tiled=True)  34.6 us
    all_to_all x1, waiting for transfers between devices, on_device(): received = jnp.concatenate(lax.all_to_all(heard, 'epoch', 0, 0), axis=1)  10.3 us
    all_to_all x1, starting transfers between devices, on_device(): received = jnp.concatenate(lax.all_to_all(heard, 'epoch', 0, 0), axis=1)  5.39 us
    unnamed x27, local copies, waits for them, and re-layouts  4.53 us
    gather x3, local copies, waits for them, and re-layouts, roll_forward(): return lax.dynamic_slice_in_dim(doubled, across, side, 1)  2.97 us
    gather x2, local copies, waits for them, and re-layouts, roll_forward(): rows = lax.dynamic_slice_in_dim(doubled, down, side, 0)  2.71 us
    another operation x1, local copies, waits for them, and re-layouts, on_device(): blocks = piece[0].reshape(count, BANDS, CUT, CUT)  1.72 us
  transfers between devices with their start and end apart: 1, of which 1 were waited for; matrix products, arithmetic and copies ran while one was open for 0% of the time, Pallas kernels for 0%

profile of v1, /device:TPU:0, one launch (start us, length us, event | category | flops | bytes accessed | tf_op | source)
XLA Modules:
  0.0 70.6 jit_solution(10355427787271316890)
XLA Ops:
  0.0 1.0 %convert_element_type.47 = bf16[1,2,6,4096]{3,1,2,0:T(2,128)(2,1)S(1)} convert(f32[1,2,6,4096]{3,1,2,0:T(2,128)} %param.10) | non-fusion elementwise | flops 49152 | bytes 294912 | tf_op jit(solution)/shard_map/convert_element_type | solution.py:60
  1.0 0.1 copy.64
  1.1 34.6 %all_gather.3 = bf16[1,16,6,4096]{3,2,0,1:T(8,128)(2,1)S(1)} all-gather(bf16[1,2,6,4096]{3,2,0,1:T(8,128)(2,1)S(1)} %copy.64), channel_id=1, replica_groups=mesh['epoch'=8,'blend'=4] {'epoch'}, dimensions={1}, use_global_device_ids=true | all-gather | bytes 884736 | tf_op jit(solution)/shard_map/all_gather | solution.py:61
  35.7 0.4 copy.65
  36.1 1.7 %reshape_squeeze.4 = bf16[16,6,64,64]{3,2,0,1:T(8,128)(2,1)S(1)} reshape(bf16[1,16,6,4096]{3,1,2,0:T(8,128)(2,1)S(1)} %copy.65) | data formatting | bytes 1572864 | tf_op jit(solution)/shard_map/reshape;squeeze | solution.py:63
  37.9 0.2 copy.91
  38.1 0.1 pad_maximum_fusion
  38.2 0.0 copy-start.3
  38.2 0.0 copy-start.4
  38.3 1.4 %gather_fusion = bf16[16,64,64]{2,0,1:T(8,128)(2,1)S(1)} fusion(bf16[16,128,64]{2,0,1:T(8,128)(2,1)S(1)} %pad_maximum_fusion, s32[16]{0:T(128)S(1)} %get-tuple-element.6), kind=kCustom, calls=%fused_computation | custom fusion | bytes 262336 | tf_op jit(solution)/shard_map/vmap()/gather | solution.py:15
  39.6 0.1 pad_maximum_fusion.3
  39.8 0.5 copy.67
  40.4 0.1 reduce.2
  40.4 0.1 reshape.82
  40.5 0.1 reduce.3
  40.5 0.1 reshape.83
  40.6 0.1 reduce
  40.7 0.1 reshape.80
  40.8 0.1 reduce.1
  40.8 0.0 copy-start.7
  40.8 0.0 copy-start.8
  40.9 0.1 reshape.81
  40.9 0.2 reshape.86
  41.2 1.4 %gather_fusion.1 = bf16[16,64,64]{1,0,2:T(8,128)(2,1)S(1)} fusion(bf16[16,64,128]{1,0,2:T(8,128)(2,1)S(1)} %copy.67, s32[16]{0:T(128)S(1)} %get-tuple-element.7), kind=kCustom, calls=%fused_computation.1 | custom fusion | bytes 262336 | tf_op jit(solution)/shard_map/vmap()/gather | solution.py:17
  42.5 0.1 fusion.10
  42.7 0.1 fusion.9
  42.8 0.4 fusion.5
  43.3 0.4 fusion.8
  43.7 0.2 pad_maximum_fusion.1
  43.9 0.5 copy.73
  44.4 1.3 %gather_fusion.2 = f32[16,64,64]{2,0,1:T(8,128)S(1)} fusion(f32[16,128,64]{2,0,1:T(8,128)S(1)} %copy.73, s32[16]{0:T(128)S(1)} %get-tuple-element.8), kind=kCustom, calls=%fused_computation.2 | custom fusion | bytes 524480 | tf_op jit(solution)/shard_map/vmap()/gather | solution.py:15
  45.8 0.2 pad_maximum_fusion.2
  46.0 0.6 copy.74
  46.6 1.3 %gather_fusion.3 = f32[16,64,64]{1,0,2:T(8,128)S(1)} fusion(f32[16,64,128]{1,0,2:T(8,128)S(1)} %copy.74, s32[16]{0:T(128)S(1)} %get-tuple-element.5), kind=kCustom, calls=%fused_computation.3 | custom fusion | bytes 524480 | tf_op jit(solution)/shard_map/vmap()/gather | solution.py:17
  47.9 0.3 copy.75
  48.2 0.2 broadcast_in_dim.5
  48.3 0.6 fusion.15
  49.0 0.6 fusion.17
  49.6 0.6 fusion.19
  50.3 0.6 fusion.21
  50.9 0.6 fusion.23
  51.5 0.6 fusion.25
  52.2 0.6 fusion.27
  52.8 0.6 fusion.29
  53.5 5.4 %all-to-all-start = ((f32[8,2,2,4096]{3,1,2,0:T(2,128)}), f32[8,2,2,4096]{3,1,2,0:T(2,128)S(1)}, u32[]{:S(2)}, u32[]{:S(2)}) async-start(f32[8,2,2,4096]{3,1,2,0:T(2,128)} %fusion.29), calls=%async_computation | async-start | bytes 1048576 | tf_op jit(solution)/shard_map/all_to_all | solution.py:72
  58.9 10.3 %all-to-all-done = f32[8,2,2,4096]{3,1,2,0:T(2,128)S(1)} async-done(((f32[8,2,2,4096]{3,1,2,0:T(2,128)}), f32[8,2,2,4096]{3,1,2,0:T(2,128)S(1)}, u32[]{:S(2)}, u32[]{:S(2)}) %all-to-all-start) | async-done | bytes 524320 | tf_op jit(solution)/shard_map/all_to_all | solution.py:72
  69.1 0.7 fusion.3
  69.8 0.8 %copy.77 = f32[1,2,6,4096]{3,1,2,0:T(2,128)} copy(f32[1,2,6,4096]{3,2,1,0:T(8,128)S(1)} %fusion.3) | data formatting | bytes 393216 | tf_op jit(solution)/shard_map/broadcast_in_dim | solution.py:81
  (21 shorter events, 0.1 us)
Async XLA Ops:
  36.1 2.1 %copy-start.6 = (s32[1,16,2]{1,2,0:T(2,128)S(1)}, s32[1,16,2]{1,2,0:T(2,128)}, u32[]{:S(2)}) copy-start(s32[1,16,2]{1,2,0:T(2,128)} %param.14) | copy-start | bytes 388
  38.2 2.1 %copy-start.2 = (bf16[1,4096]{1,0:T(2,128)(2,1)S(1)}, bf16[1,4096]{1,0:T(2,128)(2,1)}, u32[]{:S(2)}) copy-start(bf16[1,4096]{1,0:T(2,128)(2,1)} %param.18) | copy-start | bytes 24580
  38.2 2.3 %copy-start.3 = (bf16[1,4096]{1,0:T(2,128)(2,1)S(1)}, bf16[1,4096]{1,0:T(2,128)(2,1)}, u32[]{:S(2)}) copy-start(bf16[1,4096]{1,0:T(2,128)(2,1)} %param.19) | copy-start | bytes 24580
  38.2 2.4 %copy-start.4 = (bf16[1,4096]{1,0:T(2,128)(2,1)S(1)}, bf16[1,4096]{1,0:T(2,128)(2,1)}, u32[]{:S(2)}) copy-start(bf16[1,4096]{1,0:T(2,128)(2,1)} %param.16) | copy-start | bytes 24580
  38.2 2.5 %copy-start.5 = (bf16[1,4096]{1,0:T(2,128)(2,1)S(1)}, bf16[1,4096]{1,0:T(2,128)(2,1)}, u32[]{:S(2)}) copy-start(bf16[1,4096]{1,0:T(2,128)(2,1)} %param.17) | copy-start | bytes 24580
  38.3 2.7 %copy-start.1 = (bf16[1,16,4096]{2,1,0:T(8,128)(2,1)S(1)}, bf16[1,16,4096]{2,1,0:T(8,128)(2,1)}, u32[]{:S(2)}) copy-start(bf16[1,16,4096]{2,1,0:T(8,128)(2,1)} %param.11) | copy-start | bytes 393220
  40.8 2.0 %copy-start.7 = (f32[1,16]{1,0:T(1,128)S(1)}, f32[1,16]{1,0:T(1,128)}, u32[]{:S(2)}) copy-start(f32[1,16]{1,0:T(1,128)} %param.12) | copy-start | bytes 196
  40.8 1.9 %copy-start.8 = (s32[1,16]{1,0:T(1,128)S(1)}, s32[1,16]{1,0:T(1,128)}, u32[]{:S(2)}) copy-start(s32[1,16]{1,0:T(1,128)} %param.13) | copy-start | bytes 196
  49.6 9.3 %copy-start.9 = (s32[1,2]{1,0:T(1,128)S(1)}, s32[1,2]{1,0:T(1,128)}, u32[]{:S(2)}) copy-start(s32[1,2]{1,0:T(1,128)} %param.15) | copy-start | bytes 28
  49.6 19.5 %copy-start = (f32[1,2,6,4096]{3,1,2,0:T(2,128)S(1)}, f32[1,2,6,4096]{3,1,2,0:T(2,128)}, u32[]{:S(2)}) copy-start(f32[1,2,6,4096]{3,1,2,0:T(2,128)} %param.10) | copy-start | bytes 589828
  53.5 15.7 %all-to-all-start = ((f32[8,2,2,4096]{3,1,2,0:T(2,128)}), f32[8,2,2,4096]{3,1,2,0:T(2,128)S(1)}, u32[]{:S(2)}, u32[]{:S(2)}) async-start(f32[8,2,2,4096]{3,1,2,0:T(2,128)} %fusion.29), calls=%async_computation | async-start | bytes 1048576 | tf_op jit(solution)/shard_map/all_to_all | solution.py:72
